TPU v7x, 32 devices: a whole 2x2x4 slice. The times are simulated.
32 devices in a mesh: floor: 4 (over y, x), zone: 8 (over z, core).
Axes of the slice: x: 2, y: 2, z: 4, core: 2. Of those that a mesh axis runs over, the one named last changes fastest.
Arguments:
- factor: float32 [512, 96, 384], P(('floor', 'zone')), may hold values from -0.625 to 0.625
- plant_map: float32 [512, 96, 384], P(('floor', 'zone')), may hold values from -0.4082483 to 0.4082483
- offset: float32 [512, 384], P(('floor', 'zone')), may hold values from -10 to 10
- start_plan: float32 [512, 384], P(('floor', 'zone')), may hold values from -10 to 10
- demand: float32 [4, 48], replicated, may hold values from -768 to 768
- start_price: float32 [4, 48], replicated, may hold values from -6 to 6
- start_multiplier: float32 [512, 48], P(('floor', 'zone')), may hold values from -6 to 6
- neighbors: int32 [512, 4], P(('floor', 'zone')), may hold values from 0 to 127
- loop_of_zone: int32 [512], P(('floor', 'zone')), may hold values from 0 to 3
Outputs:
- control: float32 [512, 384], P(('floor', 'zone'))
- price: float32 [4, 48], replicated
- multiplier: float32 [512, 48], P(('floor', 'zone'))
Inputs may be any that keep to these rules, and one draw needn't show every extreme that they name: `neighbors`: indices count zones within the zone's own floor of 128 consecutive zones.
All inputs are finite; a program needn't handle non-finite values.
Results may differ from a plain program's by a relative error of at most 0.0001.
Values sent between devices are 32-bit elements; how exact they have to be, the bound alone decides.
No kernel may reach another device: no remote copies, remote signals or barrier semaphores. Data moves between devices by JAX's collectives and lax.ppermute only.
A program may use at most 64 MiB of HBM per device.

v0:
```python
import jax
import jax.numpy as jnp
from jax import lax
from jax.sharding import PartitionSpec as P

HORIZON = 48
NEIGHBORS = 4
LOOPS = 4
ITERS = 2


def select_rows(neighbors, count):
    columns = jnp.arange(count, dtype=jnp.int32)
    picks = (neighbors[:, :, None] == columns[None, None, :]).astype(jnp.float32)
    return jnp.sum(picks, axis=1) / NEIGHBORS


def local(
    factor,
    plant_map,
    offset,
    start_plan,
    demand,
    start_price,
    start_multiplier,
    neighbors,
    loop_of_zone,
):
    control = start_plan
    price = start_price
    multiplier = start_multiplier
    zones_here = control.shape[0]
    zones_all = zones_here * lax.axis_size("floor") * lax.axis_size("zone")
    onehot = (loop_of_zone[:, None] == jnp.arange(LOOPS, dtype=jnp.int32)[None, :]).astype(
        jnp.float32
    )
    for step in range(ITERS):
        outputs = jnp.einsum("zkv,zv->zk", plant_map, control, precision=lax.Precision.HIGHEST)
        shares = outputs[:, :HORIZON]
        bound = outputs[:, HORIZON:]
        partial_load = jnp.dot(onehot.T, shares, precision=lax.Precision.HIGHEST)
        floor_load = lax.psum(partial_load, "zone")
        total = lax.psum(floor_load, "floor")
        excess = (total - demand) * (LOOPS / zones_all)
        shift = jnp.dot(onehot, excess + price, precision=lax.Precision.HIGHEST)
        price = price + excess
        target_share = shares - shift
        floor_bound = lax.all_gather(bound, "zone", axis=0, tiled=True)
        weights = select_rows(neighbors, floor_bound.shape[0])
        near = jnp.dot(weights, floor_bound, precision=lax.Precision.HIGHEST)
        target_bound = (bound + near) / 2.0 - multiplier
        multiplier = multiplier + (bound - near) / 2.0
        target = jnp.concatenate([target_share, target_bound], axis=1)
        control = (
            0.8 * jnp.einsum("zkv,zk->zv", factor, target, precision=lax.Precision.HIGHEST) - offset
        )
    return (control, price, multiplier)


def solution(mesh):
    placed = (
        P(("floor", "zone"), None, None),
        P(("floor", "zone"), None, None),
        P(("floor", "zone"), None),
        P(("floor", "zone"), None),
        P(),
        P(),
        P(("floor", "zone"), None),
        P(("floor", "zone"), None),
        P(("floor", "zone")),
    )
    return jax.shard_map(
        local,
        mesh=mesh,
        in_specs=placed,
        out_specs=(P(("floor", "zone"), None), P(), P(("floor", "zone"), None)),
        check_vma=False,
    )
```

profile of v0, /device:TPU:0, one launch (start us, length us, event | category | flops | bytes accessed | tf_op | source)
XLA Modules:
  0.0 91.8 jit_solution(17976281189199001725)
XLA Ops:
  0.6 0.0 copy-start
  0.6 0.0 copy-start.3
  0.7 0.0 copy-start.4
  0.7 0.0 copy-start.8
  0.7 0.0 copy-start.5
  0.7 0.0 copy-start.6
  0.7 0.0 copy-start.2
  0.7 4.4 %fusion.5 = f32[16,1,96]{2,1,0:T(1,128)S(1)} fusion(f32[16,96,384]{2,1,0:T(8,128)} %param.10, f32[16,384,1]{1,0,2:T(8,128)} %bitcast.43), kind=kOutput, calls=%fused_computation.11 | convolution fusion | flops 7077888 | bytes 2390016 | tf_op jit(solution)/shard_map/zkv,zv->zk/dot_general | solution.py:38
  5.1 0.1 slice.17
  5.2 15.7 %all_gather.6 = f32[128,48]{1,0:T(8,128)S(1)} all-gather(f32[16,48]{1,0:T(8,128)S(1)} %slice.17), channel_id=1, replica_groups=mesh['floor'=4,'zone'=8] {'zone'}, dimensions={0}, use_global_device_ids=true | all-gather | bytes 27648 | tf_op jit(solution)/shard_map/all_gather | solution.py:48
  20.9 0.0 copy-done.4
  20.9 0.1 convert_reduce_fusion
  21.0 0.0 copy-done.3
  21.0 0.2 multiply_subtract_fusion.1
  21.1 0.0 copy-done.8
  21.1 0.3 fusion.8
  21.4 16.9 %psum.28 = f32[4,48]{1,0:T(4,128)S(1)} all-reduce(f32[4,48]{1,0:T(4,128)S(1)} %fusion.8), channel_id=1, replica_groups=mesh['floor'=4,'zone'=8] {'zone'}, use_global_device_ids=true, to_apply=%region_0.0 | all-reduce | flops 192 | bytes 1536 | tf_op jit(solution)/shard_map/psum | solution.py:42
  38.3 9.9 %psum.29 = f32[4,48]{1,0:T(4,128)S(1)} all-reduce(f32[4,48]{1,0:T(4,128)S(1)} %psum.28), channel_id=1, replica_groups=mesh['floor'=4,'zone'=8] {'floor'}, use_global_device_ids=true, to_apply=%region_1.0 | all-reduce | flops 192 | bytes 1536 | tf_op jit(solution)/shard_map/psum | solution.py:43
  48.2 0.2 convolution_subtract_fusion.1
  48.4 0.1 pad_maximum_fusion
  48.5 1.4 %fusion.24 = f32[16,1,384]{2,1,0:T(1,128)S(1)} fusion(f32[16,96,1]{1,2,0:T(1,128)S(1)} %bitcast.41, f32[16,96,384]{2,1,0:T(8,128)S(1)} %copy-done), kind=kOutput, calls=%fused_computation.39 | convolution fusion | flops 7077888 | bytes 2390016 | tf_op jit(solution)/shard_map/zkv,zk->zv/dot_general | solution.py:55
  49.9 2.6 %fusion.3 = f32[16,1,96]{2,1,0:T(1,128)S(1)} fusion(f32[16,96,384]{2,1,0:T(8,128)S(1)} %copy-done.1, f32[16,384,1]{1,0,2:T(8,128)S(1)} %fusion.2), kind=kOutput, calls=%fused_computation.9 | convolution fusion | flops 7077888 | bytes 2390016 | tf_op jit(solution)/shard_map/zkv,zv->zk/dot_general | solution.py:38
  52.5 0.1 slice.19
  52.6 14.0 %all_gather.7 = f32[128,48]{1,0:T(8,128)S(1)} all-gather(f32[16,48]{1,0:T(8,128)S(1)} %slice.19), channel_id=1, replica_groups=mesh['floor'=4,'zone'=8] {'zone'}, dimensions={0}, use_global_device_ids=true | all-gather | bytes 27648 | tf_op jit(solution)/shard_map/all_gather | solution.py:48
  66.6 0.8 multiply_add_fusion
  67.4 0.3 fusion.7
  67.6 13.9 %psum.30 = f32[4,48]{1,0:T(4,128)S(1)} all-reduce(f32[4,48]{1,0:T(4,128)S(1)} %fusion.7), channel_id=1, replica_groups=mesh['floor'=4,'zone'=8] {'zone'}, use_global_device_ids=true, to_apply=%region_3.0 | all-reduce | flops 192 | bytes 1536 | tf_op jit(solution)/shard_map/psum | solution.py:42
  81.5 7.9 %psum.31 = f32[4,48]{1,0:T(4,128)S(1)} all-reduce(f32[4,48]{1,0:T(4,128)S(1)} %psum.30), channel_id=1, replica_groups=mesh['floor'=4,'zone'=8] {'floor'}, use_global_device_ids=true, to_apply=%region_4.0 | all-reduce | flops 192 | bytes 1536 | tf_op jit(solution)/shard_map/psum | solution.py:43
  89.5 0.2 convolution_subtract_fusion
  89.7 0.1 pad_maximum_fusion.1
  89.8 1.4 %fusion.25 = f32[16,1,384]{2,1,0:T(1,128)S(1)} fusion(f32[16,96,1]{1,2,0:T(1,128)S(1)} %bitcast.42, f32[16,96,384]{2,1,0:T(8,128)S(1)} %copy-done), kind=kOutput, calls=%fused_computation.40 | convolution fusion | flops 7077888 | bytes 2390016 | tf_op jit(solution)/shard_map/zkv,zk->zv/dot_general | solution.py:55
  91.2 0.6 fusion
  (10 shorter events, 0.0 us)
Async XLA Ops:
  0.6 47.8 %copy-start = (f32[16,96,384]{2,1,0:T(8,128)S(1)}, f32[16,96,384]{2,1,0:T(8,128)}, u32[]{:S(2)}) copy-start(f32[16,96,384]{2,1,0:T(8,128)} %param.9) | copy-start | bytes 7077892
  0.6 20.3 %copy-start.3 = (f32[16,48]{1,0:T(8,128)S(1)}, f32[16,48]{1,0:T(8,128)}, u32[]{:S(2)}) copy-start(f32[16,48]{1,0:T(8,128)} %param.15) | copy-start | bytes 9220
  0.7 20.2 %copy-start.4 = (s32[16,4]{0,1:T(4,128)S(1)}, s32[16,4]{0,1:T(4,128)}, u32[]{:S(2)}) copy-start(s32[16,4]{0,1:T(4,128)} %param.16) | copy-start | bytes 772
  0.7 20.5 %copy-start.8 = (s32[16]{0:T(128)S(1)}, s32[16]{0:T(128)}, u32[]{:S(2)}) copy-start(s32[16]{0:T(128)} %param.17) | copy-start | bytes 196
  0.7 47.5 %copy-start.5 = (f32[4,48]{1,0:T(4,128)S(1)}, f32[4,48]{1,0:T(4,128)}, u32[]{:S(2)}) copy-start(f32[4,48]{1,0:T(4,128)} %param.14) | copy-start | bytes 2308
  0.7 47.5 %copy-start.6 = (f32[4,48]{1,0:T(4,128)S(1)}, f32[4,48]{1,0:T(4,128)}, u32[]{:S(2)}) copy-start(f32[4,48]{1,0:T(4,128)} %param.13) | copy-start | bytes 2308
  0.7 49.2 %copy-start.2 = (f32[16,384]{1,0:T(8,128)S(1)}, f32[16,384]{1,0:T(8,128)}, u32[]{:S(2)}) copy-start(f32[16,384]{1,0:T(8,128)} %param.11) | copy-start | bytes 73732
  48.2 1.7 %copy-start.1 = (f32[16,96,384]{2,1,0:T(8,128)S(1)}, f32[16,96,384]{2,1,0:T(8,128)}, u32[]{:S(2)}) copy-start(f32[16,96,384]{2,1,0:T(8,128)} %param.10) | copy-start | bytes 7077892
  89.5 2.3 %copy-start.7 = (f32[4,48]{1,0:T(4,128)}, f32[4,48]{1,0:T(4,128)S(1)}, u32[]{:S(2)}) copy-start(f32[4,48]{1,0:T(4,128)S(1)} %multiply_add_fusion.2) | copy-start | bytes 2308
where the time goes:
time: 92.1 us; the launch traced here: 91.8 us
  blocking collectives  78.3 us (85%)
  matrix products  11.7 us (13%)
    psum x2, blocking collectives, local(): floor_load = lax.psum(partial_load, 'zone')  30.8 us
    all_gather x2, blocking collectives, local(): floor_bound = lax.all_gather(bound, 'zone', axis=0, tiled=True)  29.7 us
    psum x2, blocking collectives, local(): total = lax.psum(floor_load, 'floor')  17.8 us
    dot_general x2, matrix products, local(): jnp.einsum('zkv,zv->zk', plant_map, control, precision=lax.Precision.HIGH...  7 us
    dot_general x2, matrix products, local(): jnp.einsum('zkv,zk->zv', factor, target, precision=lax.Precision.HIGHEST)  2.88 us

commit v1 on v0

--- a/solution.py
+++ b/solution.py
@@ -30,7 +30,10 @@
     price = start_price
     multiplier = start_multiplier
     zones_here = control.shape[0]
-    zones_all = zones_here * lax.axis_size("floor") * lax.axis_size("zone")
+    per_floor = lax.axis_size("zone")
+    devices = lax.axis_size("floor") * per_floor
+    floor = lax.axis_index("floor")
+    zones_all = zones_here * devices
     onehot = (loop_of_zone[:, None] == jnp.arange(LOOPS, dtype=jnp.int32)[None, :]).astype(
         jnp.float32
     )
@@ -39,13 +42,16 @@
         shares = outputs[:, :HORIZON]
         bound = outputs[:, HORIZON:]
         partial_load = jnp.dot(onehot.T, shares, precision=lax.Precision.HIGHEST)
-        floor_load = lax.psum(partial_load, "zone")
-        total = lax.psum(floor_load, "floor")
+        packed = jnp.concatenate([bound, partial_load], axis=0)
+        spread = jnp.broadcast_to(packed[None], (devices,) + packed.shape)
+        got = lax.all_to_all(spread, ("floor", "zone"), 0, 0)
+        total = jnp.sum(got[:, zones_here:], axis=0)
         excess = (total - demand) * (LOOPS / zones_all)
         shift = jnp.dot(onehot, excess + price, precision=lax.Precision.HIGHEST)
         price = price + excess
         target_share = shares - shift
-        floor_bound = lax.all_gather(bound, "zone", axis=0, tiled=True)
+        own_floor = lax.dynamic_slice_in_dim(got, floor * per_floor, per_floor, 0)
+        floor_bound = own_floor[:, :zones_here].reshape(per_floor * zones_here, HORIZON)
         weights = select_rows(neighbors, floor_bound.shape[0])
         near = jnp.dot(weights, floor_bound, precision=lax.Precision.HIGHEST)
         target_bound = (bound + near) / 2.0 - multiplier

time: 92.1 us -> 43.4 us (0.47)
  blocking collectives: 78.3 us -> 9.86 us
  waiting for transfers between devices: 0 us -> 8.07 us
  starting transfers between devices: 0 us -> 7.33 us
  local copies, waits for them, and re-layouts: 0.2 us -> 2.49 us
  other arithmetic: 0.87 us -> 2.87 us
    psum x4 -> x0, blocking collectives: 48.6 us -> none  [the longest x2 30.8 us: local(): floor_load = lax.psum(partial_load, 'zone')]
    all_gather x2 -> x0, blocking collectives: 29.7 us -> none  [local(): floor_bound = lax.all_gather(bound, 'zone', axis=0, tiled=True)]
    all_to_all x0 -> x1, blocking collectives: none -> 9.86 us  [local(): got = lax.all_to_all(spread, ('floor', 'zone'), 0, 0)]
    all_to_all x0 -> x1, waiting for transfers between devices: none -> 8.07 us  [local(): got = lax.all_to_all(spread, ('floor', 'zone'), 0, 0)]
    all_to_all x0 -> x1, starting transfers between devices: none -> 7.33 us  [local(): got = lax.all_to_all(spread, ('floor', 'zone'), 0, 0)]
    all_to_all x0 -> x2, other arithmetic: none -> 1.9 us  [local(): got = lax.all_to_all(spread, ('floor', 'zone'), 0, 0)]
    unnamed x18 -> x22, local copies, waits for them, and re-layouts: 0.05 us -> 1.75 us
  transfers between devices with their start and end apart: 0 -> 1, of which waited for: 0 -> 1; matrix products, arithmetic and copies ran while one was open for 0% -> 0% of each run, Pallas kernels for 0% -> 0%
where the time goes in v1:
time: 43.4 us; the launch traced here: 43.2 us
  matrix products  11.7 us (27%)
  blocking collectives  9.86 us (23%)
  waiting for transfers between devices  8.07 us (19%)
  starting transfers between devices  7.33 us (17%)
  other arithmetic  2.87 us (7%)
  local copies, waits for them, and re-layouts  2.49 us (6%)
  between operations  0.86 us (2%)
    all_to_all x1, blocking collectives, local(): got = lax.all_to_all(spread, ('floor', 'zone'), 0, 0)  9.86 us
    all_to_all x1, waiting for transfers between devices, local(): got = lax.all_to_all(spread, ('floor', 'zone'), 0, 0)  8.07 us
    all_to_all x1, starting transfers between devices, local(): got = lax.all_to_all(spread, ('floor', 'zone'), 0, 0)  7.33 us
    dot_general x2, matrix products, local(): jnp.einsum('zkv,zv->zk', plant_map, control, precision=lax.Precision.HIGH...  7 us
    dot_general x2, matrix products, local(): jnp.einsum('zkv,zk->zv', factor, target, precision=lax.Precision.HIGHEST)  2.87 us
    all_to_all x2, other arithmetic, local(): got = lax.all_to_all(spread, ('floor', 'zone'), 0, 0)  1.9 us
    unnamed x22, local copies, waits for them, and re-layouts  1.75 us
    dot_general x2, matrix products, local(): near = jnp.dot(weights, floor_bound, precision=lax.Precision.HIGHEST)  0.94 us
  transfers between devices with their start and end apart: 1, of which 1 were waited for; matrix products, arithmetic and copies ran while one was open for 0% of the time, Pallas kernels for 0%

profile of v1, /device:TPU:0, one launch (start us, length us, event | category | flops | bytes accessed | tf_op | source)
XLA Modules:
  0.0 43.2 jit_solution(1202833921639382469)
XLA Ops:
  0.6 0.0 copy-start
  0.7 4.4 %fusion.5 = f32[16,1,96]{2,1,0:T(1,128)S(1)} fusion(f32[16,96,384]{2,1,0:T(8,128)} %param.10, f32[16,384,1]{1,0,2:T(8,128)} %bitcast.47), kind=kOutput, calls=%fused_computation.13 | convolution fusion | flops 7077888 | bytes 2390016 | tf_op jit(solution)/shard_map/zkv,zv->zk/dot_general | solution.py:41
  5.1 0.1 slice.33
  5.2 0.3 fusion.8
  5.5 0.0 copy-start.2
  5.5 1.0 %reshape.26 = f32[32,1,960]{2,1,0:T(1,128)} reshape(f32[32,20,48]{2,1,0:T(8,128)S(1)} %broadcast_in_dim.4) | data formatting | bytes 245760
  6.5 7.3 %all-to-all-start = ((f32[32,1,960]{2,1,0:T(1,128)}), f32[32,1,960]{2,1,0:T(1,128)S(1)}, u32[]{:S(2)}, u32[]{:S(2)}) async-start(f32[32,1,960]{2,1,0:T(1,128)} %reshape.26), calls=%async_computation | async-start | bytes 262144 | tf_op jit(solution)/shard_map/all_to_all | solution.py:47
  13.9 0.1 convert_reduce_fusion
  13.9 8.1 %all-to-all-done = f32[32,1,960]{2,1,0:T(1,128)S(1)} async-done(((f32[32,1,960]{2,1,0:T(1,128)}), f32[32,1,960]{2,1,0:T(1,128)S(1)}, u32[]{:S(2)}, u32[]{:S(2)}) %all-to-all-start) | async-done | bytes 122912 | tf_op jit(solution)/shard_map/all_to_all | solution.py:47
  22.0 0.5 %broadcast.52 = f32[]{:T(128)} broadcast(f32[]{:T(128)} %constant.57), dimensions={} | broadcast | bytes 8 | tf_op jit(solution)/shard_map/all_to_all | solution.py:47
  22.5 0.9 %reduce = f32[32,960]{1,0:T(8,128)S(1)} reduce(f32[32,1,960]{2,1,0:T(1,128)S(1)} %all-to-all-done, f32[]{:T(128)} %broadcast.52), dimensions={1}, to_apply=%all_to_all.6.reduce_sub_computation | reduce | bytes 245764 | tf_op jit(solution)/shard_map/all_to_all | solution.py:47
  23.5 0.2 reshape.27
  23.6 0.0 copy-start.1
  23.7 0.0 copy-done.3
  23.7 0.2 multiply_subtract_fusion.1
  23.9 0.0 copy-done.5
  23.9 0.2 convolution_subtract_fusion.1
  24.1 0.1 pad_maximum_fusion.2
  24.2 1.4 %fusion.24 = f32[16,1,384]{2,1,0:T(1,128)S(1)} fusion(f32[16,96,1]{1,2,0:T(1,128)S(1)} %bitcast.45, f32[16,96,384]{2,1,0:T(8,128)S(1)} %copy-done), kind=kOutput, calls=%fused_computation.45 | convolution fusion | flops 7077888 | bytes 2390016 | tf_op jit(solution)/shard_map/zkv,zk->zv/dot_general | solution.py:61
  25.7 2.6 %fusion.3 = f32[16,1,96]{2,1,0:T(1,128)S(1)} fusion(f32[16,96,384]{2,1,0:T(8,128)S(1)} %copy-done.1, f32[16,384,1]{1,0,2:T(8,128)S(1)} %fusion.2), kind=kOutput, calls=%fused_computation.11 | convolution fusion | flops 7077888 | bytes 2390016 | tf_op jit(solution)/shard_map/zkv,zv->zk/dot_general | solution.py:41
  28.2 0.3 fusion.7
  28.5 0.1 slice.36
  28.6 0.4 reshape.28
  29.0 9.9 %all_to_all.10 = f32[32,1,960]{2,1,0:T(1,128)S(1)} all-to-all(f32[32,1,960]{2,1,0:T(1,128)S(1)} %reshape.28), channel_id=1, replica_groups=mesh['floor'=4,'zone'=8] {'floor','zone'}, dimensions={0} | all-to-all | bytes 245760 | tf_op jit(solution)/shard_map/all_to_all | solution.py:47
  38.9 1.0 %reduce.1 = f32[32,960]{1,0:T(8,128)S(1)} reduce(f32[32,1,960]{2,1,0:T(1,128)S(1)} %all_to_all.10, f32[]{:T(128)} %broadcast.52), dimensions={1}, to_apply=%all_to_all.7.reduce_sub_computation | reduce | bytes 245764 | tf_op jit(solution)/shard_map/all_to_all | solution.py:47
  39.8 0.2 reshape.29
  40.1 0.0 copy-start.7
  40.1 0.2 convolution_subtract_fusion
  40.3 0.8 %multiply_add_fusion = (f32[16,48]{1,0:T(8,128)}, f32[16,48]{1,0:T(8,128)S(1)}) fusion(f32[16,96]{1,0:T(8,128)S(1)} %bitcast.44, f32[16,48]{1,0:T(8,128)S(1)} %copy-done.3, f32[16,48]{1,0:T(8,128)S(1)} %get-tuple-element.6, f32[16,96]{1,0:T(8,128)S(1)} %bitcast.40, f32[128,48]{1,0:T(8,128)S(1)} %bitcast.34, f32[16,128]{1,0:T(8,128)S(1)} %convert_reduce_fusion), kind=kOutput, calls=%fused_computation.19 | convolution fusion | flops 1188608 | bytes 51200 | tf_op jit(solution)/shard_map/dot_general | solution.py:56
  41.1 0.1 pad_maximum_fusion.3
  41.1 1.4 %fusion.25 = f32[16,1,384]{2,1,0:T(1,128)S(1)} fusion(f32[16,96,1]{1,2,0:T(1,128)S(1)} %bitcast.46, f32[16,96,384]{2,1,0:T(8,128)S(1)} %copy-done), kind=kOutput, calls=%fused_computation.46 | convolution fusion | flops 7077888 | bytes 2390016 | tf_op jit(solution)/shard_map/zkv,zk->zv/dot_general | solution.py:61
  42.6 0.6 %fusion = f32[16,384]{1,0:T(8,128)} fusion(f32[16,384]{1,0:T(8,128)S(1)} %copy-done.2, f32[16,1,384]{2,1,0:T(1,128)S(1)} %fusion.25), kind=kLoop, calls=%fused_computation.7 | loop fusion | flops 12288 | bytes 73728 | tf_op jit(solution)/shard_map/sub | solution.py:61
  (22 shorter events, 0.2 us)
Async XLA Ops:
  0.6 23.5 %copy-start = (f32[16,96,384]{2,1,0:T(8,128)S(1)}, f32[16,96,384]{2,1,0:T(8,128)}, u32[]{:S(2)}) copy-start(f32[16,96,384]{2,1,0:T(8,128)} %param.9) | copy-start | bytes 7077892
  0.6 4.5 %copy-start.8 = (s32[16]{0:T(128)S(1)}, s32[16]{0:T(128)}, u32[]{:S(2)}) copy-start(s32[16]{0:T(128)} %param.17) | copy-start | bytes 196
  0.7 13.2 %copy-start.4 = (s32[16,4]{0,1:T(4,128)S(1)}, s32[16,4]{0,1:T(4,128)}, u32[]{:S(2)}) copy-start(s32[16,4]{0,1:T(4,128)} %param.16) | copy-start | bytes 772
  0.7 23.0 %copy-start.3 = (f32[16,48]{1,0:T(8,128)S(1)}, f32[16,48]{1,0:T(8,128)}, u32[]{:S(2)}) copy-start(f32[16,48]{1,0:T(8,128)} %param.15) | copy-start | bytes 9220
  0.7 23.2 %copy-start.5 = (f32[4,48]{1,0:T(4,128)S(1)}, f32[4,48]{1,0:T(4,128)}, u32[]{:S(2)}) copy-start(f32[4,48]{1,0:T(4,128)} %param.14) | copy-start | bytes 2308
  0.7 23.2 %copy-start.6 = (f32[4,48]{1,0:T(4,128)S(1)}, f32[4,48]{1,0:T(4,128)}, u32[]{:S(2)}) copy-start(f32[4,48]{1,0:T(4,128)} %param.13) | copy-start | bytes 2308
  5.5 20.2 %copy-start.2 = (f32[16,384]{1,0:T(8,128)S(1)}, f32[16,384]{1,0:T(8,128)}, u32[]{:S(2)}) copy-start(f32[16,384]{1,0:T(8,128)} %param.11) | copy-start | bytes 73732
  6.5 15.5 %all-to-all-start = ((f32[32,1,960]{2,1,0:T(1,128)}), f32[32,1,960]{2,1,0:T(1,128)S(1)}, u32[]{:S(2)}, u32[]{:S(2)}) async-start(f32[32,1,960]{2,1,0:T(1,128)} %reshape.26), calls=%async_computation | async-start | bytes 262144 | tf_op jit(solution)/shard_map/all_to_all | solution.py:47
  23.6 2.0 %copy-start.1 = (f32[16,96,384]{2,1,0:T(8,128)S(1)}, f32[16,96,384]{2,1,0:T(8,128)}, u32[]{:S(2)}) copy-start(f32[16,96,384]{2,1,0:T(8,128)} %param.10) | copy-start | bytes 7077892
  40.1 3.1 %copy-start.7 = (f32[4,48]{1,0:T(4,128)}, f32[4,48]{1,0:T(4,128)S(1)}, u32[]{:S(2)}) copy-start(f32[4,48]{1,0:T(4,128)S(1)} %multiply_add_fusion.2) | copy-start | bytes 2308

commit v2 on v1

v2 whole, which is shorter than its diff:
```python
import functools

import jax
import jax.numpy as jnp
from jax import lax
from jax.experimental import pallas as pl
from jax.experimental.pallas import tpu as pltpu
from jax.sharding import PartitionSpec as P

LOOPS = 4
ITERS = 2
LANES = 128
EXACT = lax.Precision.HIGHEST


def iota(shape, dim):
    return lax.broadcasted_iota(jnp.int32, shape, dim)


def dot(a, b):
    return jnp.dot(a, b, precision=EXACT, preferred_element_type=jnp.float32)


def dot_rows(a, b):
    return lax.dot_general(
        a, b, (((0,), (0,)), ((), ())), precision=EXACT, preferred_element_type=jnp.float32
    )


def members(loop, rows):
    return (iota((rows, loop.shape[1]), 0) == loop).astype(jnp.float32)


def outputs_of(maps, control, zones, wide):
    lane = iota((wide, LANES), 1)
    columns = jnp.zeros((wide, LANES), jnp.float32)
    controls = control.shape[1]
    for z in range(zones):
        row = control[z : z + 1]
        block = maps(z)
        part = block[:, :LANES] * row[:, :LANES]
        for v in range(LANES, controls, LANES):
            part = part + block[:, v : v + LANES] * row[:, v : v + LANES]
        columns = jnp.where(lane == z, jnp.sum(part, axis=1, keepdims=True), columns)
    square = jnp.concatenate([columns, jnp.zeros((LANES - wide, LANES), jnp.float32)], axis=0)
    return square.T[:zones]


def decide(factor, target, zones, wide):
    square = jnp.concatenate([target, jnp.zeros((LANES - zones, LANES), jnp.float32)], axis=0)
    columns = square.T[:wide]
    rows = []
    for z in range(zones):
        rows.append(jnp.sum(factor(z) * columns[:, z : z + 1], axis=0, keepdims=True))
    return 0.8 * jnp.concatenate(rows, axis=0)


def pack(out, loop, horizon, zones):
    half = zones // 2
    loads = dot(members(loop, half), out)
    lane = iota((half, LANES), 1)
    row = iota((half, LANES), 0)
    first = pltpu.roll(out[:half], LANES - horizon, 1)
    rest = LANES - 2 * horizon
    ahead = pltpu.roll(loads, 2 * horizon, 1)
    behind = pltpu.roll(pltpu.roll(loads, 2 * horizon - rest, 1), LOOPS, 0)
    block = jnp.where(lane < horizon, first, out[half:])
    return jnp.where(lane < 2 * horizon, block, jnp.where(row < LOOPS, ahead, behind))


def total_of(got_ref, horizon):
    total = jnp.sum(got_ref[...], axis=0)
    rest = LANES - 2 * horizon
    lane = iota(total.shape, 1)
    ahead = pltpu.roll(total, LANES - 2 * horizon, 1)
    behind = pltpu.roll(pltpu.roll(total, LANES - 2 * horizon + rest, 1), total.shape[0] - LOOPS, 0)
    return jnp.where(lane < rest, ahead, behind)


def near_of(got_ref, neighbors, per_floor, horizon, zones):
    half = zones // 2
    own = got_ref[pl.ds(lax.axis_index("floor") * per_floor, per_floor)].reshape(per_floor * half, LANES)
    column = iota((per_floor * half, zones), 0)
    low = (column // half) * zones + column % half
    count = neighbors.shape[0]
    pick_low = jnp.zeros(column.shape, jnp.float32)
    pick_high = pick_low
    for b in range(count):
        which = neighbors[b : b + 1]
        pick_low = pick_low + (which == low).astype(jnp.float32)
        pick_high = pick_high + (which == low + half).astype(jnp.float32)
    return (pltpu.roll(dot_rows(pick_low, own), horizon, 1) + dot_rows(pick_high, own)) / count


def widen(ref, scratch, shift):
    scratch[...] = jnp.zeros_like(scratch)
    scratch[: ref.shape[0], : ref.shape[1]] = ref[...]
    value = scratch[...]
    return pltpu.roll(value, shift, 1) if shift else value


def consensus(got_ref, out, price, multiplier, demand, neighbors, loop, per_floor, scale, horizon):
    zones = out.shape[0]
    lane = iota((zones, LANES), 1)
    excess = (total_of(got_ref, horizon) - demand) * scale
    shift = dot_rows(members(loop, price.shape[0]), excess + price)
    near = near_of(got_ref, neighbors, per_floor, horizon, zones)
    target = jnp.where(lane < horizon, out - shift, (out + near) / 2.0 - multiplier)
    return target, price + excess, multiplier + (out - near) / 2.0


def first_kernel(horizon, map_ref, plan_ref, loop_ref, out_ref, send_ref):
    zones, wide = map_ref.shape[0], map_ref.shape[1]
    out = outputs_of(lambda z: map_ref[z], plan_ref[...], zones, wide)
    out_ref[...] = out
    block = pack(out, loop_ref[...], horizon, zones)
    send_ref[...] = jnp.broadcast_to(block[None], send_ref.shape)


def middle_kernel(
    per_floor, scale, horizon,
    got_ref, out_ref, price_ref, mult_ref, demand_ref, nb_ref, loop_ref,
    offset_ref, factor_ref, map_ref,
    next_out_ref, next_price_ref, next_mult_ref, send_ref, wide8, wide16,
):
    zones, wide = map_ref.shape[0], map_ref.shape[1]
    target, price, mult = consensus(
        got_ref, out_ref[...], widen(price_ref, wide8, 0), widen(mult_ref, wide16, horizon),
        widen(demand_ref, wide8, 0), nb_ref[...], loop_ref[...], per_floor, scale, horizon,
    )
    next_price_ref[...] = price
    next_mult_ref[...] = mult
    control = decide(lambda z: factor_ref[z], target, zones, wide) - offset_ref[...]
    out = outputs_of(lambda z: map_ref[z], control, zones, wide)
    next_out_ref[...] = out
    block = pack(out, loop_ref[...], horizon, zones)
    send_ref[...] = jnp.broadcast_to(block[None], send_ref.shape)


def last_kernel(
    per_floor, scale, horizon,
    got_ref, out_ref, price_ref, mult_ref, demand_ref, nb_ref, loop_ref, offset_ref, factor_ref,
    control_ref, next_price_ref, next_mult_ref, wide8,
):
    zones, wide = factor_ref.shape[0], factor_ref.shape[1]
    target, price, mult = consensus(
        got_ref, out_ref[...], price_ref[...], mult_ref[...], widen(demand_ref, wide8, 0),
        nb_ref[...], loop_ref[...], per_floor, scale, horizon,
    )
    next_price_ref[...] = price[: next_price_ref.shape[0], :horizon]
    next_mult_ref[...] = pltpu.roll(mult, LANES - horizon, 1)[:, :horizon]
    control_ref[...] = decide(lambda z: factor_ref[z], target, zones, wide) - offset_ref[...]


def local(
    factor, plant_map, offset, start_plan, demand, start_price, start_multiplier, neighbors, loop_of_zone
):
    zones, wide, controls = plant_map.shape
    horizon = wide // 2
    half = zones // 2
    per_floor = lax.axis_size("zone")
    devices = lax.axis_size("floor") * per_floor
    scale = LOOPS / (zones * devices)
    loop_row = loop_of_zone[None, :]
    neighbors = neighbors.T
    vmem = pl.BlockSpec(memory_space=pltpu.VMEM)
    f32 = jnp.float32
    rows = jax.ShapeDtypeStruct((zones, LANES), f32)
    send = jax.ShapeDtypeStruct((devices, half, LANES), f32)
    eight = jax.ShapeDtypeStruct((half, LANES), f32)
    params = pltpu.CompilerParams(vmem_limit_bytes=24 * 1024 * 1024)

    out, spread = pl.pallas_call(
        functools.partial(first_kernel, horizon),
        out_shape=(rows, send),
        in_specs=[vmem] * 3,
        out_specs=(vmem, vmem),
        compiler_params=params,
        name="first",
    )(plant_map, start_plan, loop_row)
    price, multiplier = start_price, start_multiplier
    for step in range(ITERS - 1):
        got = lax.all_to_all(spread, ("floor", "zone"), 0, 0)
        out, price, multiplier, spread = pl.pallas_call(
            functools.partial(middle_kernel, per_floor, scale, horizon),
            out_shape=(rows, eight, rows, send),
            in_specs=[vmem] * 10,
            out_specs=(vmem,) * 4,
            scratch_shapes=[pltpu.VMEM((half, LANES), f32), pltpu.VMEM((zones, LANES), f32)],
            compiler_params=params,
            name="middle",
        )(
            got, out, price, multiplier, demand, neighbors, loop_row,
            offset, factor, plant_map,
        )
    got = lax.all_to_all(spread, ("floor", "zone"), 0, 0)
    return pl.pallas_call(
        functools.partial(last_kernel, per_floor, scale, horizon),
        out_shape=(
            jax.ShapeDtypeStruct((zones, controls), f32),
            jax.ShapeDtypeStruct(start_price.shape, f32),
            jax.ShapeDtypeStruct(start_multiplier.shape, f32),
        ),
        in_specs=[vmem] * 9,
        out_specs=(vmem,) * 3,
        scratch_shapes=[pltpu.VMEM((half, LANES), f32)],
        compiler_params=params,
        name="last",
    )(got, out, price, multiplier, demand, neighbors, loop_row, offset, factor)


def solution(mesh):
    placed = (
        P(("floor", "zone"), None, None),
        P(("floor", "zone"), None, None),
        P(("floor", "zone"), None),
        P(("floor", "zone"), None),
        P(),
        P(),
        P(("floor", "zone"), None),
        P(("floor", "zone"), None),
        P(("floor", "zone")),
    )
    return jax.shard_map(
        local,
        mesh=mesh,
        in_specs=placed,
        out_specs=(P(("floor", "zone"), None), P(), P(("floor", "zone"), None)),
        check_vma=False,
    )
```

time: 43.4 us -> 32.5 us (0.75)
  blocking collectives: 9.86 us -> 25.2 us
  matrix products: 11.7 us -> 0 us
  waiting for transfers between devices: 8.07 us -> 0 us
  starting transfers between devices: 7.33 us -> 0 us
  Pallas kernels: 0 us -> 3.33 us
  other arithmetic: 2.87 us -> 0 us
  local copies, waits for them, and re-layouts: 2.49 us -> 3.08 us
    all_to_all x1 -> x2, blocking collectives: 9.86 us -> 25.2 us  [local(): got = lax.all_to_all(spread, ('floor', 'zone'), 0, 0)]
    dot_general x10 -> x0, matrix products: 11.7 us -> none  [the longest x2 7 us: local(): jnp.einsum('zkv,zv->zk', plant_map, control, precision=lax.Precision.HIGH...]
    all_to_all x1 -> x0, waiting for transfers between devices: 8.07 us -> none  [local(): got = lax.all_to_all(spread, ('floor', 'zone'), 0, 0)]
    all_to_all x1 -> x0, starting transfers between devices: 7.33 us -> none  [local(): got = lax.all_to_all(spread, ('floor', 'zone'), 0, 0)]
    pallas_call x0 -> x3, Pallas kernels: none -> 3.33 us  [the longest x1 1.44 us: local(): pl.pallas_call(functools.partial(last_kernel, per_floor, scale, horizon),...]
    all_to_all x2 -> x0, other arithmetic: 1.9 us -> none  [local(): got = lax.all_to_all(spread, ('floor', 'zone'), 0, 0)]
    unnamed x22 -> x20, local copies, waits for them, and re-layouts: 1.75 us -> 3.08 us
    sub x2 -> x0, other arithmetic: 0.63 us -> none  [local(): 0.8 * jnp.einsum('zkv,zk->zv', factor, target, precision=lax.Precision.HI...]
  transfers between devices with their start and end apart: 1 -> 0, of which waited for: 1 -> 0; matrix products, arithmetic and copies ran while one was open for 0% -> 0% of each run, Pallas kernels for 0% -> 0%
where the time goes in v2:
time: 32.5 us; the launch traced here: 32.3 us
  blocking collectives  25.2 us (78%)
  Pallas kernels  3.33 us (10%)
  local copies, waits for them, and re-layouts  3.08 us (9%)
  between operations  0.72 us (2%)
    all_to_all x2, blocking collectives, local(): got = lax.all_to_all(spread, ('floor', 'zone'), 0, 0)  25.2 us
    unnamed x20, local copies, waits for them, and re-layouts  3.08 us
    pallas_call x1, Pallas kernels, local(): pl.pallas_call(functools.partial(last_kernel, per_floor, scale, horizon),...  1.44 us
    pallas_call x1, Pallas kernels, local(): pl.pallas_call(functools.partial(middle_kernel, per_floor, scale, horizon...  1.36 us

profile of v2, /device:TPU:0, one launch (start us, length us, event | category | flops | bytes accessed | tf_op | source)
XLA Modules:
  0.0 32.3 jit_solution(14987796356135235077)
XLA Ops:
  0.6 0.0 copy-start
  0.6 1.7 %copy-done = f32[16,96,384]{2,1,0:T(8,128)S(1)} copy-done((f32[16,96,384]{2,1,0:T(8,128)S(1)}, f32[16,96,384]{2,1,0:T(8,128)}, u32[]{:S(2)}) %copy-start) | copy-done | bytes 2359320
  2.3 0.0 copy-start.3
  2.3 0.7 %copy-done.3 = f32[16,384]{1,0:T(8,128)S(1)} copy-done((f32[16,384]{1,0:T(8,128)S(1)}, f32[16,384]{1,0:T(8,128)}, u32[]{:S(2)}) %copy-start.3) | copy-done | bytes 24600
  3.0 0.0 copy-start.7
  3.0 0.7 %copy-done.7 = s32[16]{0:T(128)S(1)} copy-done((s32[16]{0:T(128)S(1)}, s32[16]{0:T(128)}, u32[]{:S(2)}) %copy-start.7) | copy-done | bytes 88
  3.7 0.0 copy-start.1
  3.7 0.0 copy-start.2
  3.7 0.0 copy-start.4
  3.7 0.0 copy-start.5
  3.7 0.0 copy-start.6
  3.7 0.0 copy-start.9
  3.7 0.5 %first.1 = (f32[16,128]{1,0:T(8,128)S(1)}, f32[32,8,128]{2,1,0:T(8,128)S(1)}) custom-call(f32[16,96,384]{2,1,0:T(8,128)S(1)} %copy-done, f32[16,384]{1,0:T(8,128)S(1)} %copy-done.3, s32[1,16]{1,0:T(1,128)S(1)} %bitcast.4), custom_call_target="tpu_custom_call" | custom-call | tf_op jit(solution)/shard_map/first/pallas_call | solution.py:173
  4.3 15.3 %all_to_all.10.got_ref = f32[32,8,128]{2,1,0:T(8,128)S(1)} all-to-all(f32[32,8,128]{2,1,0:T(8,128)S(1)} %get-tuple-element.9), channel_id=1, replica_groups=mesh['floor'=4,'zone'=8] {'floor','zone'}, dimensions={0} | all-to-all | bytes 262144 | tf_op jit(solution)/shard_map/all_to_all | solution.py:183
  19.6 0.0 copy-done.1
  19.6 0.0 copy-done.2
  19.6 0.0 copy-done.4
  19.6 0.0 copy-done.5
  19.6 0.0 copy-done.6
  19.6 0.0 copy-done.9
  19.6 0.0 copy-start.8
  19.6 1.4 %middle.1 = (f32[16,128]{1,0:T(8,128)S(1)}, f32[8,128]{1,0:T(8,128)S(1)}, f32[16,128]{1,0:T(8,128)S(1)}, f32[32,8,128]{2,1,0:T(8,128)S(1)}) custom-call(f32[32,8,128]{2,1,0:T(8,128)S(1)} %all_to_all.10.got_ref, f32[16,128]{1,0:T(8,128)S(1)} %get-tuple-element.10.out_ref, f32[4,48]{1,0:T(4,128)S(1)} %copy-done.9, f32[16,48]{1,0:T(8,128)S(1)} %copy-done.4, ...), custom_call_target="tpu_custom_call" | custom-call | tf_op jit(solution)/shard_map/middle/pallas_call | solution.py:184
  21.0 9.9 %all_to_all.11.got_ref = f32[32,8,128]{2,1,0:T(8,128)S(1)} all-to-all(f32[32,8,128]{2,1,0:T(8,128)S(1)} %get-tuple-element.11), channel_id=1, replica_groups=mesh['floor'=4,'zone'=8] {'floor','zone'}, dimensions={0} | all-to-all | bytes 262144 | tf_op jit(solution)/shard_map/all_to_all | solution.py:196
  30.8 0.0 copy-done.8
  30.8 1.4 %last.1 = (f32[16,384]{1,0:T(8,128)}, f32[4,48]{1,0:T(4,128)}, f32[16,48]{1,0:T(8,128)}) custom-call(f32[32,8,128]{2,1,0:T(8,128)S(1)} %all_to_all.11.got_ref, f32[16,128]{1,0:T(8,128)S(1)} %get-tuple-element.12.out_ref, f32[8,128]{1,0:T(8,128)S(1)} %get-tuple-element.13.price_ref, f32[16,128]{1,0:T(8,128)S(1)} %get-tuple-element.14.mult_ref, ...), custom_call_target="tpu_custom_call" | custom-call | tf_op jit(solution)/shard_map/last/pallas_call | solution.py:197
Async XLA Ops:
  0.6 1.7 %copy-start = (f32[16,96,384]{2,1,0:T(8,128)S(1)}, f32[16,96,384]{2,1,0:T(8,128)}, u32[]{:S(2)}) copy-start(f32[16,96,384]{2,1,0:T(8,128)} %map_ref.3) | copy-start | bytes 7077892
  2.3 0.7 %copy-start.3 = (f32[16,384]{1,0:T(8,128)S(1)}, f32[16,384]{1,0:T(8,128)}, u32[]{:S(2)}) copy-start(f32[16,384]{1,0:T(8,128)} %plan_ref.1) | copy-start | bytes 73732
  3.0 0.7 %copy-start.7 = (s32[16]{0:T(128)S(1)}, s32[16]{0:T(128)}, u32[]{:S(2)}) copy-start(s32[16]{0:T(128)} %param.17) | copy-start | bytes 196
  3.7 15.9 %copy-start.1 = (f32[16,96,384]{2,1,0:T(8,128)S(1)}, f32[16,96,384]{2,1,0:T(8,128)}, u32[]{:S(2)}) copy-start(f32[16,96,384]{2,1,0:T(8,128)} %factor_ref.3) | copy-start | bytes 7077892
  3.7 15.9 %copy-start.2 = (f32[16,384]{1,0:T(8,128)S(1)}, f32[16,384]{1,0:T(8,128)}, u32[]{:S(2)}) copy-start(f32[16,384]{1,0:T(8,128)} %offset_ref.3) | copy-start | bytes 73732
  3.7 15.9 %copy-start.4 = (f32[16,48]{1,0:T(8,128)S(1)}, f32[16,48]{1,0:T(8,128)}, u32[]{:S(2)}) copy-start(f32[16,48]{1,0:T(8,128)} %mult_ref.1) | copy-start | bytes 9220
  3.7 15.9 %copy-start.5 = (f32[4,48]{1,0:T(4,128)S(1)}, f32[4,48]{1,0:T(4,128)}, u32[]{:S(2)}) copy-start(f32[4,48]{1,0:T(4,128)} %demand_ref.3) | copy-start | bytes 2308
  3.7 15.9 %copy-start.6 = (s32[16,4]{0,1:T(4,128)S(1)}, s32[16,4]{0,1:T(4,128)}, u32[]{:S(2)}) copy-start(s32[16,4]{0,1:T(4,128)} %param.16) | copy-start | bytes 772
  3.7 15.9 %copy-start.9 = (f32[4,48]{1,0:T(4,128)S(1)}, f32[4,48]{1,0:T(4,128)}, u32[]{:S(2)}) copy-start(f32[4,48]{1,0:T(4,128)} %price_ref.1) | copy-start | bytes 2308
  19.6 11.2 %copy-start.8 = (s32[16]{0:T(128)S(1)}, s32[16]{0:T(128)}, u32[]{:S(2)}) copy-start(s32[16]{0:T(128)} %param.17) | copy-start | bytes 196

commit v3 on v2

--- a/solution.py
+++ b/solution.py
@@ -55,9 +55,9 @@
     return 0.8 * jnp.concatenate(rows, axis=0)
 
 
-def pack(out, loop, horizon, zones):
+def pack(out, loop, rows, horizon, zones):
     half = zones // 2
-    loads = dot(members(loop, half), out)
+    loads = dot((rows[:, :zones] == loop).astype(jnp.float32), out)
     lane = iota((half, LANES), 1)
     row = iota((half, LANES), 0)
     first = pltpu.roll(out[:half], LANES - horizon, 1)
@@ -109,11 +109,15 @@
     return target, price + excess, multiplier + (out - near) / 2.0
 
 
-def first_kernel(horizon, map_ref, plan_ref, loop_ref, out_ref, send_ref):
+def index_kernel(rows_ref):
+    rows_ref[...] = iota(rows_ref.shape, 0)
+
+
+def first_kernel(horizon, map_ref, plan_ref, loop_ref, rows_ref, out_ref, send_ref):
     zones, wide = map_ref.shape[0], map_ref.shape[1]
     out = outputs_of(lambda z: map_ref[z], plan_ref[...], zones, wide)
     out_ref[...] = out
-    block = pack(out, loop_ref[...], horizon, zones)
+    block = pack(out, loop_ref[...], rows_ref[...], horizon, zones)
     send_ref[...] = jnp.broadcast_to(block[None], send_ref.shape)
 
 
@@ -133,7 +137,7 @@
     control = decide(lambda z: factor_ref[z], target, zones, wide) - offset_ref[...]
     out = outputs_of(lambda z: map_ref[z], control, zones, wide)
     next_out_ref[...] = out
-    block = pack(out, loop_ref[...], horizon, zones)
+    block = pack(out, loop_ref[...], iota((zones // 2, LANES), 0), horizon, zones)
     send_ref[...] = jnp.broadcast_to(block[None], send_ref.shape)
 
 
@@ -170,14 +174,24 @@
     eight = jax.ShapeDtypeStruct((half, LANES), f32)
     params = pltpu.CompilerParams(vmem_limit_bytes=24 * 1024 * 1024)
 
+    row_index = pl.pallas_call(
+        index_kernel,
+        out_shape=jax.ShapeDtypeStruct((half, LANES), jnp.int32),
+        out_specs=vmem,
+        compiler_params=params,
+        cost_estimate=pl.CostEstimate(
+            flops=4000 * plant_map.size, bytes_accessed=80 * plant_map.size, transcendentals=0
+        ),
+        name="index",
+    )()
     out, spread = pl.pallas_call(
         functools.partial(first_kernel, horizon),
         out_shape=(rows, send),
-        in_specs=[vmem] * 3,
+        in_specs=[vmem] * 4,
         out_specs=(vmem, vmem),
         compiler_params=params,
         name="first",
-    )(plant_map, start_plan, loop_row)
+    )(plant_map, start_plan, loop_row, row_index)
     price, multiplier = start_price, start_multiplier
     for step in range(ITERS - 1):
         got = lax.all_to_all(spread, ("floor", "zone"), 0, 0)

time: 32.5 us -> 31 us (0.954)
  local copies, waits for them, and re-layouts: 3.08 us -> 1.6 us
    unnamed x20 -> x18, local copies, waits for them, and re-layouts: 3.08 us -> 1.6 us
where the time goes in v3:
time: 31 us; the launch traced here: 30.9 us
  blocking collectives  25.2 us (81%)
  Pallas kernels  3.37 us (11%)
  local copies, waits for them, and re-layouts  1.6 us (5%)
  between operations  0.76 us (2%)
    all_to_all x2, blocking collectives, local(): got = lax.all_to_all(spread, ('floor', 'zone'), 0, 0)  25.2 us
    unnamed x18, local copies, waits for them, and re-layouts  1.6 us
    pallas_call x1, Pallas kernels, local(): pl.pallas_call(functools.partial(last_kernel, per_floor, scale, horizon),...  1.44 us
    pallas_call x1, Pallas kernels, local(): pl.pallas_call(functools.partial(middle_kernel, per_floor, scale, horizon...  1.37 us

profile of v3, /device:TPU:0, one launch (start us, length us, event | category | flops | bytes accessed | tf_op | source)
XLA Modules:
  0.0 30.9 jit_solution(10212924011372074257)
XLA Ops:
  0.6 0.0 copy-start
  0.6 0.0 copy-start.7
  0.7 0.0 copy-start.3
  0.7 0.0 copy-start.1
  0.7 0.0 copy-start.2
  0.7 0.0 copy-start.4
  0.7 0.0 copy-start.5
  0.7 0.0 copy-start.6
  0.7 0.0 copy-start.8
  0.7 1.6 %copy-done = f32[16,96,384]{2,1,0:T(8,128)S(1)} copy-done((f32[16,96,384]{2,1,0:T(8,128)S(1)}, f32[16,96,384]{2,1,0:T(8,128)}, u32[]{:S(2)}) %copy-start) | copy-done | bytes 2359320
  2.3 0.0 copy-done.7
  2.3 0.0 copy-done.3
  2.3 0.6 %first.1 = (f32[16,128]{1,0:T(8,128)S(1)}, f32[32,8,128]{2,1,0:T(8,128)S(1)}) custom-call(f32[16,96,384]{2,1,0:T(8,128)S(1)} %copy-done, f32[16,384]{1,0:T(8,128)S(1)} %copy-done.3, s32[1,16]{1,0:T(1,128)S(1)} %bitcast.4, s32[8,128]{1,0:T(8,128)S(1)} %index.1.rows_ref), custom_call_target="tpu_custom_call" | custom-call | tf_op jit(solution)/shard_map/first/pallas_call | solution.py:187
  2.9 15.3 %all_to_all.10.got_ref = f32[32,8,128]{2,1,0:T(8,128)S(1)} all-to-all(f32[32,8,128]{2,1,0:T(8,128)S(1)} %get-tuple-element.9), channel_id=1, replica_groups=mesh['floor'=4,'zone'=8] {'floor','zone'}, dimensions={0} | all-to-all | bytes 262144 | tf_op jit(solution)/shard_map/all_to_all | solution.py:197
  18.2 0.0 copy-done.1
  18.2 0.0 copy-done.2
  18.2 0.0 copy-done.4
  18.2 0.0 copy-done.5
  18.2 0.0 copy-done.6
  18.2 0.0 copy-done.8
  18.2 1.4 %middle.1 = (f32[16,128]{1,0:T(8,128)S(1)}, f32[8,128]{1,0:T(8,128)S(1)}, f32[16,128]{1,0:T(8,128)S(1)}, f32[32,8,128]{2,1,0:T(8,128)S(1)}) custom-call(f32[32,8,128]{2,1,0:T(8,128)S(1)} %all_to_all.10.got_ref, f32[16,128]{1,0:T(8,128)S(1)} %get-tuple-element.10.out_ref, f32[4,48]{1,0:T(4,128)S(1)} %copy-done.8, f32[16,48]{1,0:T(8,128)S(1)} %copy-done.4, ...), custom_call_target="tpu_custom_call" | custom-call | tf_op jit(solution)/shard_map/middle/pallas_call | solution.py:198
  19.6 9.9 %all_to_all.11.got_ref = f32[32,8,128]{2,1,0:T(8,128)S(1)} all-to-all(f32[32,8,128]{2,1,0:T(8,128)S(1)} %get-tuple-element.11), channel_id=1, replica_groups=mesh['floor'=4,'zone'=8] {'floor','zone'}, dimensions={0} | all-to-all | bytes 262144 | tf_op jit(solution)/shard_map/all_to_all | solution.py:210
  29.4 1.4 %last.1 = (f32[16,384]{1,0:T(8,128)}, f32[4,48]{1,0:T(4,128)}, f32[16,48]{1,0:T(8,128)}) custom-call(f32[32,8,128]{2,1,0:T(8,128)S(1)} %all_to_all.11.got_ref, f32[16,128]{1,0:T(8,128)S(1)} %get-tuple-element.12.out_ref, f32[8,128]{1,0:T(8,128)S(1)} %get-tuple-element.13.price_ref, f32[16,128]{1,0:T(8,128)S(1)} %get-tuple-element.14.mult_ref, ...), custom_call_target="tpu_custom_call" | custom-call | tf_op jit(solution)/shard_map/last/pallas_call | solution.py:211
  (1 shorter events, 0.0 us)
Async XLA Ops:
  0.6 1.7 %copy-start = (f32[16,96,384]{2,1,0:T(8,128)S(1)}, f32[16,96,384]{2,1,0:T(8,128)}, u32[]{:S(2)}) copy-start(f32[16,96,384]{2,1,0:T(8,128)} %map_ref.3) | copy-start | bytes 7077892
  0.6 1.7 %copy-start.7 = (s32[16]{0:T(128)S(1)}, s32[16]{0:T(128)}, u32[]{:S(2)}) copy-start(s32[16]{0:T(128)} %param.17) | copy-start | bytes 196
  0.7 1.7 %copy-start.3 = (f32[16,384]{1,0:T(8,128)S(1)}, f32[16,384]{1,0:T(8,128)}, u32[]{:S(2)}) copy-start(f32[16,384]{1,0:T(8,128)} %plan_ref.1) | copy-start | bytes 73732
  0.7 17.5 %copy-start.1 = (f32[16,96,384]{2,1,0:T(8,128)S(1)}, f32[16,96,384]{2,1,0:T(8,128)}, u32[]{:S(2)}) copy-start(f32[16,96,384]{2,1,0:T(8,128)} %factor_ref.3) | copy-start | bytes 7077892
  0.7 17.5 %copy-start.2 = (f32[16,384]{1,0:T(8,128)S(1)}, f32[16,384]{1,0:T(8,128)}, u32[]{:S(2)}) copy-start(f32[16,384]{1,0:T(8,128)} %offset_ref.3) | copy-start | bytes 73732
  0.7 17.5 %copy-start.4 = (f32[16,48]{1,0:T(8,128)S(1)}, f32[16,48]{1,0:T(8,128)}, u32[]{:S(2)}) copy-start(f32[16,48]{1,0:T(8,128)} %mult_ref.1) | copy-start | bytes 9220
  0.7 17.5 %copy-start.5 = (f32[4,48]{1,0:T(4,128)S(1)}, f32[4,48]{1,0:T(4,128)}, u32[]{:S(2)}) copy-start(f32[4,48]{1,0:T(4,128)} %demand_ref.3) | copy-start | bytes 2308
  0.7 17.5 %copy-start.6 = (s32[16,4]{0,1:T(4,128)S(1)}, s32[16,4]{0,1:T(4,128)}, u32[]{:S(2)}) copy-start(s32[16,4]{0,1:T(4,128)} %param.16) | copy-start | bytes 772
  0.7 17.5 %copy-start.8 = (f32[4,48]{1,0:T(4,128)S(1)}, f32[4,48]{1,0:T(4,128)}, u32[]{:S(2)}) copy-start(f32[4,48]{1,0:T(4,128)} %price_ref.1) | copy-start | bytes 2308
